TPU v7x, 64 devices: a 2x2x8 block of a 4x4x8 slice. The times are simulated.
64 devices in a mesh: data: 4 (over x, y), ctx: 16 (over z, core).
Axes of the slice: x: 2, y: 2, z: 8, core: 2. Of those that a mesh axis runs over, the one named last changes fastest.
The devices are a block of a 4x4x8 slice.
Arguments:
- queries: bfloat16 [4, 8192, 16, 128], P('data', 'ctx'), parts along dimension 0
- keys_in: bfloat16 [4, 8192, 4, 128], P('data', 'ctx'), parts along dimension 0
- values_in: bfloat16 [4, 8192, 4, 128], P('data', 'ctx'), parts along dimension 0
- grad_out: bfloat16 [4, 8192, 16, 128], P('data', 'ctx'), parts along dimension 0
Outputs:
- output 1: bfloat16 [4, 8192, 16, 128], P('data', 'ctx'), parts along dimension 0
- output 2: bfloat16 [4, 8192, 16, 128], P('data', 'ctx'), parts along dimension 0
- output 3: bfloat16 [4, 8192, 4, 128], P('data', 'ctx'), parts along dimension 0
- output 4: bfloat16 [4, 8192, 4, 128], P('data', 'ctx'), parts along dimension 0
There are 4 independent parts. A program takes and returns all parts, laid end to end along the dimension named above; each array names one.
All inputs are finite; a program needn't handle non-finite values.
Results may differ from a plain program's by a relative error of at most 0.0169614.
Values are sent between devices in bfloat16 or wider.
A program may use at most 768 MiB of HBM per device.

v0:
```python
import jax
import jax.numpy as jnp
from jax import lax
from jax.sharding import PartitionSpec as P

MASK_VALUE = -1e30


def solution(mesh):
    ctx_size = mesh.shape["ctx"]
    block_spec = P("data", "ctx", None, None)
    perm_next = [(dev_id, (dev_id + 1) % ctx_size) for dev_id in range(ctx_size)]

    def local_attention(queries, keys_in, values_in, grad_out):
        batch_size, shard_len, q_heads, head_dim = queries.shape
        kv_heads = keys_in.shape[2]
        group_size = q_heads // kv_heads
        half_len = shard_len // 2
        score_scale = head_dim ** -0.5
        my_index = lax.axis_index("ctx")
        q_five = queries.reshape(batch_size, shard_len, kv_heads, group_size, head_dim)
        g_five = grad_out.reshape(batch_size, shard_len, kv_heads, group_size, head_dim)
        own_mask = jnp.arange(shard_len)[:, None] >= jnp.arange(shard_len)[None, :]

        def scores_of(q_blk, k_blk, mask_tile):
            raw_scores = jnp.einsum("bqhgd,bkhd->bhgqk", q_blk, k_blk, preferred_element_type=jnp.float32) * score_scale
            if mask_tile is None:
                return raw_scores
            return jnp.where(mask_tile, raw_scores, MASK_VALUE)

        def fwd_update(run_state, q_blk, k_blk, v_blk, mask_tile):
            run_max, run_sum, acc_out = run_state
            scores = scores_of(q_blk, k_blk, mask_tile)
            new_max = jnp.maximum(run_max, jnp.max(scores, axis=-1))
            prob_tile = jnp.exp(scores - new_max[..., None])
            decay_factor = jnp.exp(run_max - new_max)
            new_sum = run_sum * decay_factor + jnp.sum(prob_tile, axis=-1)
            pv_part = jnp.einsum("bhgqk,bkhd->bhgqd", prob_tile.astype(jnp.bfloat16), v_blk, preferred_element_type=jnp.float32)
            return new_max, new_sum, acc_out * decay_factor[..., None] + pv_part

        def fwd_past(op_args):
            run_state, k_cur, v_cur = op_args
            return fwd_update(run_state, q_five, k_cur[:, :half_len], v_cur[:, :half_len], None)

        def fwd_future(op_args):
            run_state, k_cur, v_cur = op_args
            low_half = tuple(tensor[:, :, :, :half_len] for tensor in run_state)
            high_half = tuple(tensor[:, :, :, half_len:] for tensor in run_state)
            high_half = fwd_update(high_half, q_five[:, half_len:], k_cur, v_cur, None)
            return tuple(jnp.concatenate([low_part, high_part], axis=3) for low_part, high_part in zip(low_half, high_half))

        def fwd_step(step_idx, loop_carry):
            k_cur, v_cur, run_state = loop_carry
            k_cur = lax.ppermute(k_cur, "ctx", perm_next)
            v_cur = lax.ppermute(v_cur, "ctx", perm_next)
            source_id = (my_index - step_idx) % ctx_size
            run_state = lax.cond(source_id < my_index, fwd_past, fwd_future, (run_state, k_cur, v_cur))
            return k_cur, v_cur, run_state

        stat_shape = (batch_size, kv_heads, group_size, shard_len)
        run_state = (jnp.full(stat_shape, MASK_VALUE, jnp.float32), jnp.zeros(stat_shape, jnp.float32), jnp.zeros(stat_shape + (head_dim,), jnp.float32))
        run_state = fwd_update(run_state, q_five, keys_in, values_in, own_mask)
        loop_out = lax.fori_loop(1, ctx_size, fwd_step, (keys_in, values_in, run_state))
        run_max, run_sum, acc_out = loop_out[2]
        out_heads = (acc_out / run_sum[..., None]).astype(jnp.bfloat16)
        log_sum = run_max + jnp.log(run_sum)
        attn_out = jnp.transpose(out_heads, (0, 3, 1, 2, 4)).reshape(batch_size, shard_len, q_heads, head_dim)
        d_rows = jnp.einsum("bqhgd,bhgqd->bhgq", g_five, out_heads, preferred_element_type=jnp.float32)

        def bwd_block(q_blk, g_blk, lse_blk, drow_blk, k_blk, v_blk, mask_tile):
            prob_tile = jnp.exp(scores_of(q_blk, k_blk, mask_tile) - lse_blk[..., None])
            grad_v = jnp.einsum("bhgqk,bqhgd->bkhd", prob_tile.astype(jnp.bfloat16), g_blk, preferred_element_type=jnp.float32)
            dprob_tile = jnp.einsum("bqhgd,bkhd->bhgqk", g_blk, v_blk, preferred_element_type=jnp.float32)
            dscore_tile = (prob_tile * (dprob_tile - drow_blk[..., None])).astype(jnp.bfloat16)
            grad_q = jnp.einsum("bhgqk,bkhd->bqhgd", dscore_tile, k_blk, preferred_element_type=jnp.float32) * score_scale
            grad_k = jnp.einsum("bhgqk,bqhgd->bkhd", dscore_tile, q_blk, preferred_element_type=jnp.float32) * score_scale
            return grad_q, grad_k, grad_v

        def bwd_past(op_args):
            dq_acc, dk_acc, dv_acc, k_cur, v_cur = op_args
            grad_q, grad_k, grad_v = bwd_block(q_five, g_five, log_sum, d_rows, k_cur[:, :half_len], v_cur[:, :half_len], None)
            dk_acc = jnp.concatenate([dk_acc[:, :half_len] + grad_k, dk_acc[:, half_len:]], axis=1)
            dv_acc = jnp.concatenate([dv_acc[:, :half_len] + grad_v, dv_acc[:, half_len:]], axis=1)
            return dq_acc + grad_q, dk_acc, dv_acc

        def bwd_future(op_args):
            dq_acc, dk_acc, dv_acc, k_cur, v_cur = op_args
            grad_q, grad_k, grad_v = bwd_block(q_five[:, half_len:], g_five[:, half_len:], log_sum[..., half_len:], d_rows[..., half_len:], k_cur, v_cur, None)
            dq_acc = jnp.concatenate([dq_acc[:, :half_len], dq_acc[:, half_len:] + grad_q], axis=1)
            return dq_acc, dk_acc + grad_k, dv_acc + grad_v

        def bwd_step(step_idx, loop_carry):
            dq_acc, dk_acc, dv_acc, k_cur, v_cur = loop_carry
            k_cur = lax.ppermute(k_cur, "ctx", perm_next)
            v_cur = lax.ppermute(v_cur, "ctx", perm_next)
            dk_acc = lax.ppermute(dk_acc, "ctx", perm_next)
            dv_acc = lax.ppermute(dv_acc, "ctx", perm_next)
            source_id = (my_index - step_idx) % ctx_size
            dq_acc, dk_acc, dv_acc = lax.cond(source_id < my_index, bwd_past, bwd_future, (dq_acc, dk_acc, dv_acc, k_cur, v_cur))
            return dq_acc, dk_acc, dv_acc, k_cur, v_cur

        first_grads = bwd_block(q_five, g_five, log_sum, d_rows, keys_in, values_in, own_mask)
        loop_out = lax.fori_loop(1, ctx_size, bwd_step, first_grads + (keys_in, values_in))
        grad_k = lax.ppermute(loop_out[1], "ctx", perm_next)
        grad_v = lax.ppermute(loop_out[2], "ctx", perm_next)
        grad_q = loop_out[0].reshape(batch_size, shard_len, q_heads, head_dim).astype(jnp.bfloat16)
        return attn_out, grad_q, grad_k.astype(jnp.bfloat16), grad_v.astype(jnp.bfloat16)

    return jax.shard_map(local_attention, mesh=mesh, in_specs=(block_spec,) * 4, out_specs=(block_spec,) * 4, check_vma=False)
```

profile of v0, /device:TPU:150, one launch (start us, length us, event | category | flops | bytes accessed | tf_op | source)
XLA Modules:
  0.0 1339.8 jit_solution(12531760234782292812)
XLA Ops:
  31.9 416.5 %while.46 = (s32[]{:T(128)}, bf16[1,512,4,128]{3,1,2,0:T(8,128)(2,1)}, bf16[1,512,4,128]{3,1,2,0:T(8,128)(2,1)}, f32[1,4,4,512]{3,2,1,0:T(4,128)S(1)}, f32[1,4,4...) while((s32[]{:T(128)}, ...), condition=%wide.region_9.10_spmd, body=%wide.region_2.9_spmd.sunk | while | flops 1092644864 | bytes 76546552 | solution.py:63
  486.3 834.3 %while.47 = (s32[]{:T(128)}, f32[1,512,4,4,128]{4,1,3,2,0:T(8,128)}, f32[1,512,4,128]{3,1,2,0:T(8,128)}, f32[1,512,4,128]{3,1,2,0:T(8,128)}, bf16[1,512,4,128]{3...) while((s32[]{:T(128)}, ...), condition=%wide.region_13.14_spmd, body=%wide.region_10.13_spmd.sunk | while | flops 2704146432 | bytes 120423088 | solution.py:103
  486.8 32.0 %collective-permute-done.2 = bf16[1,512,4,128]{3,1,2,0:T(8,128)(2,1)S(1)} collective-permute-done((bf16[1,512,4,128]{3,1,2,0:T(8,128)(2,1)}, bf16[1,512,4,128]{3,1,2,0:T(8,128)(2,1)S(1)}, u32[]{:S(2)}, u32[]{:S(2)}) %collective-permute-start.2) | collective-permute-done | bytes 524320 | tf_op jit(solution)/shard_map/while/body/eval_jaxpr/ppermute | solution.py:94
  525.2 18.3 %conditional.5 = (f32[1,512,4,4,128]{4,1,3,2,0:T(8,128)}, f32[1,512,4,128]{3,1,2,0:T(8,128)}, f32[1,512,4,128]{3,1,2,0:T(8,128)}) conditional(s32[]{:T(128)} %convert_element_type.133, (f32[1,512,4,4,128]{4,1,3,2,0:T(8,128)}, bf16[1,512,4,128]{3,1,2,0:T(8,128)(2,1)S(1)}, bf16[1,512,4,4,128]{4,1,3,2,0:T(8,128)(2,1)S(1)}, ...), branch_computations={%region_11.11_spmd, %region_12.12_spmd} | conditional | flops 2704146432 | bytes 105742448 | solution.py:99
  543.7 32.2 %collective-permute-done.2 = bf16[1,512,4,128]{3,1,2,0:T(8,128)(2,1)S(1)} collective-permute-done((bf16[1,512,4,128]{3,1,2,0:T(8,128)(2,1)}, bf16[1,512,4,128]{3,1,2,0:T(8,128)(2,1)S(1)}, u32[]{:S(2)}, u32[]{:S(2)}) %collective-permute-start.2) | collective-permute-done | bytes 524320 | tf_op jit(solution)/shard_map/while/body/eval_jaxpr/ppermute | solution.py:94
  582.3 18.3 %conditional.5 = (f32[1,512,4,4,128]{4,1,3,2,0:T(8,128)}, f32[1,512,4,128]{3,1,2,0:T(8,128)}, f32[1,512,4,128]{3,1,2,0:T(8,128)}) conditional(s32[]{:T(128)} %convert_element_type.133, (f32[1,512,4,4,128]{4,1,3,2,0:T(8,128)}, bf16[1,512,4,128]{3,1,2,0:T(8,128)(2,1)S(1)}, bf16[1,512,4,4,128]{4,1,3,2,0:T(8,128)(2,1)S(1)}, ...), branch_computations={%region_11.11_spmd, %region_12.12_spmd} | conditional | flops 2704146432 | bytes 105742448 | solution.py:99
  600.7 32.2 %collective-permute-done.2 = bf16[1,512,4,128]{3,1,2,0:T(8,128)(2,1)S(1)} collective-permute-done((bf16[1,512,4,128]{3,1,2,0:T(8,128)(2,1)}, bf16[1,512,4,128]{3,1,2,0:T(8,128)(2,1)S(1)}, u32[]{:S(2)}, u32[]{:S(2)}) %collective-permute-start.2) | collective-permute-done | bytes 524320 | tf_op jit(solution)/shard_map/while/body/eval_jaxpr/ppermute | solution.py:94
  639.3 18.3 %conditional.5 = (f32[1,512,4,4,128]{4,1,3,2,0:T(8,128)}, f32[1,512,4,128]{3,1,2,0:T(8,128)}, f32[1,512,4,128]{3,1,2,0:T(8,128)}) conditional(s32[]{:T(128)} %convert_element_type.133, (f32[1,512,4,4,128]{4,1,3,2,0:T(8,128)}, bf16[1,512,4,128]{3,1,2,0:T(8,128)(2,1)S(1)}, bf16[1,512,4,4,128]{4,1,3,2,0:T(8,128)(2,1)S(1)}, ...), branch_computations={%region_11.11_spmd, %region_12.12_spmd} | conditional | flops 2704146432 | bytes 105742448 | solution.py:99
  657.8 32.2 %collective-permute-done.2 = bf16[1,512,4,128]{3,1,2,0:T(8,128)(2,1)S(1)} collective-permute-done((bf16[1,512,4,128]{3,1,2,0:T(8,128)(2,1)}, bf16[1,512,4,128]{3,1,2,0:T(8,128)(2,1)S(1)}, u32[]{:S(2)}, u32[]{:S(2)}) %collective-permute-start.2) | collective-permute-done | bytes 524320 | tf_op jit(solution)/shard_map/while/body/eval_jaxpr/ppermute | solution.py:94
  696.4 18.3 %conditional.5 = (f32[1,512,4,4,128]{4,1,3,2,0:T(8,128)}, f32[1,512,4,128]{3,1,2,0:T(8,128)}, f32[1,512,4,128]{3,1,2,0:T(8,128)}) conditional(s32[]{:T(128)} %convert_element_type.133, (f32[1,512,4,4,128]{4,1,3,2,0:T(8,128)}, bf16[1,512,4,128]{3,1,2,0:T(8,128)(2,1)S(1)}, bf16[1,512,4,4,128]{4,1,3,2,0:T(8,128)(2,1)S(1)}, ...), branch_computations={%region_11.11_spmd, %region_12.12_spmd} | conditional | flops 2704146432 | bytes 105742448 | solution.py:99
  714.8 32.2 %collective-permute-done.2 = bf16[1,512,4,128]{3,1,2,0:T(8,128)(2,1)S(1)} collective-permute-done((bf16[1,512,4,128]{3,1,2,0:T(8,128)(2,1)}, bf16[1,512,4,128]{3,1,2,0:T(8,128)(2,1)S(1)}, u32[]{:S(2)}, u32[]{:S(2)}) %collective-permute-start.2) | collective-permute-done | bytes 524320 | tf_op jit(solution)/shard_map/while/body/eval_jaxpr/ppermute | solution.py:94
  753.4 18.3 %conditional.5 = (f32[1,512,4,4,128]{4,1,3,2,0:T(8,128)}, f32[1,512,4,128]{3,1,2,0:T(8,128)}, f32[1,512,4,128]{3,1,2,0:T(8,128)}) conditional(s32[]{:T(128)} %convert_element_type.133, (f32[1,512,4,4,128]{4,1,3,2,0:T(8,128)}, bf16[1,512,4,128]{3,1,2,0:T(8,128)(2,1)S(1)}, bf16[1,512,4,4,128]{4,1,3,2,0:T(8,128)(2,1)S(1)}, ...), branch_computations={%region_11.11_spmd, %region_12.12_spmd} | conditional | flops 2704146432 | bytes 105742448 | solution.py:99
  771.9 32.2 %collective-permute-done.2 = bf16[1,512,4,128]{3,1,2,0:T(8,128)(2,1)S(1)} collective-permute-done((bf16[1,512,4,128]{3,1,2,0:T(8,128)(2,1)}, bf16[1,512,4,128]{3,1,2,0:T(8,128)(2,1)S(1)}, u32[]{:S(2)}, u32[]{:S(2)}) %collective-permute-start.2) | collective-permute-done | bytes 524320 | tf_op jit(solution)/shard_map/while/body/eval_jaxpr/ppermute | solution.py:94
  810.5 18.3 %conditional.5 = (f32[1,512,4,4,128]{4,1,3,2,0:T(8,128)}, f32[1,512,4,128]{3,1,2,0:T(8,128)}, f32[1,512,4,128]{3,1,2,0:T(8,128)}) conditional(s32[]{:T(128)} %convert_element_type.133, (f32[1,512,4,4,128]{4,1,3,2,0:T(8,128)}, bf16[1,512,4,128]{3,1,2,0:T(8,128)(2,1)S(1)}, bf16[1,512,4,4,128]{4,1,3,2,0:T(8,128)(2,1)S(1)}, ...), branch_computations={%region_11.11_spmd, %region_12.12_spmd} | conditional | flops 2704146432 | bytes 105742448 | solution.py:99
  828.9 32.2 %collective-permute-done.2 = bf16[1,512,4,128]{3,1,2,0:T(8,128)(2,1)S(1)} collective-permute-done((bf16[1,512,4,128]{3,1,2,0:T(8,128)(2,1)}, bf16[1,512,4,128]{3,1,2,0:T(8,128)(2,1)S(1)}, u32[]{:S(2)}, u32[]{:S(2)}) %collective-permute-start.2) | collective-permute-done | bytes 524320 | tf_op jit(solution)/shard_map/while/body/eval_jaxpr/ppermute | solution.py:94
  867.5 18.3 %conditional.5 = (f32[1,512,4,4,128]{4,1,3,2,0:T(8,128)}, f32[1,512,4,128]{3,1,2,0:T(8,128)}, f32[1,512,4,128]{3,1,2,0:T(8,128)}) conditional(s32[]{:T(128)} %convert_element_type.133, (f32[1,512,4,4,128]{4,1,3,2,0:T(8,128)}, bf16[1,512,4,128]{3,1,2,0:T(8,128)(2,1)S(1)}, bf16[1,512,4,4,128]{4,1,3,2,0:T(8,128)(2,1)S(1)}, ...), branch_computations={%region_11.11_spmd, %region_12.12_spmd} | conditional | flops 2704146432 | bytes 105742448 | solution.py:99
  886.0 32.2 %collective-permute-done.2 = bf16[1,512,4,128]{3,1,2,0:T(8,128)(2,1)S(1)} collective-permute-done((bf16[1,512,4,128]{3,1,2,0:T(8,128)(2,1)}, bf16[1,512,4,128]{3,1,2,0:T(8,128)(2,1)S(1)}, u32[]{:S(2)}, u32[]{:S(2)}) %collective-permute-start.2) | collective-permute-done | bytes 524320 | tf_op jit(solution)/shard_map/while/body/eval_jaxpr/ppermute | solution.py:94
  924.6 18.3 %conditional.5 = (f32[1,512,4,4,128]{4,1,3,2,0:T(8,128)}, f32[1,512,4,128]{3,1,2,0:T(8,128)}, f32[1,512,4,128]{3,1,2,0:T(8,128)}) conditional(s32[]{:T(128)} %convert_element_type.133, (f32[1,512,4,4,128]{4,1,3,2,0:T(8,128)}, bf16[1,512,4,128]{3,1,2,0:T(8,128)(2,1)S(1)}, bf16[1,512,4,4,128]{4,1,3,2,0:T(8,128)(2,1)S(1)}, ...), branch_computations={%region_11.11_spmd, %region_12.12_spmd} | conditional | flops 2704146432 | bytes 105742448 | solution.py:99
  943.0 32.2 %collective-permute-done.2 = bf16[1,512,4,128]{3,1,2,0:T(8,128)(2,1)S(1)} collective-permute-done((bf16[1,512,4,128]{3,1,2,0:T(8,128)(2,1)}, bf16[1,512,4,128]{3,1,2,0:T(8,128)(2,1)S(1)}, u32[]{:S(2)}, u32[]{:S(2)}) %collective-permute-start.2) | collective-permute-done | bytes 524320 | tf_op jit(solution)/shard_map/while/body/eval_jaxpr/ppermute | solution.py:94
  981.6 15.2 %conditional.5 = (f32[1,512,4,4,128]{4,1,3,2,0:T(8,128)}, f32[1,512,4,128]{3,1,2,0:T(8,128)}, f32[1,512,4,128]{3,1,2,0:T(8,128)}) conditional(s32[]{:T(128)} %convert_element_type.133, (f32[1,512,4,4,128]{4,1,3,2,0:T(8,128)}, bf16[1,512,4,128]{3,1,2,0:T(8,128)(2,1)S(1)}, bf16[1,512,4,4,128]{4,1,3,2,0:T(8,128)(2,1)S(1)}, ...), branch_computations={%region_11.11_spmd, %region_12.12_spmd} | conditional | flops 2704146432 | bytes 105742448 | solution.py:99
  996.9 32.2 %collective-permute-done.2 = bf16[1,512,4,128]{3,1,2,0:T(8,128)(2,1)S(1)} collective-permute-done((bf16[1,512,4,128]{3,1,2,0:T(8,128)(2,1)}, bf16[1,512,4,128]{3,1,2,0:T(8,128)(2,1)S(1)}, u32[]{:S(2)}, u32[]{:S(2)}) %collective-permute-start.2) | collective-permute-done | bytes 524320 | tf_op jit(solution)/shard_map/while/body/eval_jaxpr/ppermute | solution.py:94
  1035.5 15.2 %conditional.5 = (f32[1,512,4,4,128]{4,1,3,2,0:T(8,128)}, f32[1,512,4,128]{3,1,2,0:T(8,128)}, f32[1,512,4,128]{3,1,2,0:T(8,128)}) conditional(s32[]{:T(128)} %convert_element_type.133, (f32[1,512,4,4,128]{4,1,3,2,0:T(8,128)}, bf16[1,512,4,128]{3,1,2,0:T(8,128)(2,1)S(1)}, bf16[1,512,4,4,128]{4,1,3,2,0:T(8,128)(2,1)S(1)}, ...), branch_computations={%region_11.11_spmd, %region_12.12_spmd} | conditional | flops 2704146432 | bytes 105742448 | solution.py:99
  1050.9 32.2 %collective-permute-done.2 = bf16[1,512,4,128]{3,1,2,0:T(8,128)(2,1)S(1)} collective-permute-done((bf16[1,512,4,128]{3,1,2,0:T(8,128)(2,1)}, bf16[1,512,4,128]{3,1,2,0:T(8,128)(2,1)S(1)}, u32[]{:S(2)}, u32[]{:S(2)}) %collective-permute-start.2) | collective-permute-done | bytes 524320 | tf_op jit(solution)/shard_map/while/body/eval_jaxpr/ppermute | solution.py:94
  1089.5 15.2 %conditional.5 = (f32[1,512,4,4,128]{4,1,3,2,0:T(8,128)}, f32[1,512,4,128]{3,1,2,0:T(8,128)}, f32[1,512,4,128]{3,1,2,0:T(8,128)}) conditional(s32[]{:T(128)} %convert_element_type.133, (f32[1,512,4,4,128]{4,1,3,2,0:T(8,128)}, bf16[1,512,4,128]{3,1,2,0:T(8,128)(2,1)S(1)}, bf16[1,512,4,4,128]{4,1,3,2,0:T(8,128)(2,1)S(1)}, ...), branch_computations={%region_11.11_spmd, %region_12.12_spmd} | conditional | flops 2704146432 | bytes 105742448 | solution.py:99
  1104.8 32.2 %collective-permute-done.2 = bf16[1,512,4,128]{3,1,2,0:T(8,128)(2,1)S(1)} collective-permute-done((bf16[1,512,4,128]{3,1,2,0:T(8,128)(2,1)}, bf16[1,512,4,128]{3,1,2,0:T(8,128)(2,1)S(1)}, u32[]{:S(2)}, u32[]{:S(2)}) %collective-permute-start.2) | collective-permute-done | bytes 524320 | tf_op jit(solution)/shard_map/while/body/eval_jaxpr/ppermute | solution.py:94
  1143.4 15.2 %conditional.5 = (f32[1,512,4,4,128]{4,1,3,2,0:T(8,128)}, f32[1,512,4,128]{3,1,2,0:T(8,128)}, f32[1,512,4,128]{3,1,2,0:T(8,128)}) conditional(s32[]{:T(128)} %convert_element_type.133, (f32[1,512,4,4,128]{4,1,3,2,0:T(8,128)}, bf16[1,512,4,128]{3,1,2,0:T(8,128)(2,1)S(1)}, bf16[1,512,4,4,128]{4,1,3,2,0:T(8,128)(2,1)S(1)}, ...), branch_computations={%region_11.11_spmd, %region_12.12_spmd} | conditional | flops 2704146432 | bytes 105742448 | solution.py:99
  1158.7 32.2 %collective-permute-done.2 = bf16[1,512,4,128]{3,1,2,0:T(8,128)(2,1)S(1)} collective-permute-done((bf16[1,512,4,128]{3,1,2,0:T(8,128)(2,1)}, bf16[1,512,4,128]{3,1,2,0:T(8,128)(2,1)S(1)}, u32[]{:S(2)}, u32[]{:S(2)}) %collective-permute-start.2) | collective-permute-done | bytes 524320 | tf_op jit(solution)/shard_map/while/body/eval_jaxpr/ppermute | solution.py:94
  1197.3 15.2 %conditional.5 = (f32[1,512,4,4,128]{4,1,3,2,0:T(8,128)}, f32[1,512,4,128]{3,1,2,0:T(8,128)}, f32[1,512,4,128]{3,1,2,0:T(8,128)}) conditional(s32[]{:T(128)} %convert_element_type.133, (f32[1,512,4,4,128]{4,1,3,2,0:T(8,128)}, bf16[1,512,4,128]{3,1,2,0:T(8,128)(2,1)S(1)}, bf16[1,512,4,4,128]{4,1,3,2,0:T(8,128)(2,1)S(1)}, ...), branch_computations={%region_11.11_spmd, %region_12.12_spmd} | conditional | flops 2704146432 | bytes 105742448 | solution.py:99
  1212.7 32.2 %collective-permute-done.2 = bf16[1,512,4,128]{3,1,2,0:T(8,128)(2,1)S(1)} collective-permute-done((bf16[1,512,4,128]{3,1,2,0:T(8,128)(2,1)}, bf16[1,512,4,128]{3,1,2,0:T(8,128)(2,1)S(1)}, u32[]{:S(2)}, u32[]{:S(2)}) %collective-permute-start.2) | collective-permute-done | bytes 524320 | tf_op jit(solution)/shard_map/while/body/eval_jaxpr/ppermute | solution.py:94
  1251.2 15.2 %conditional.5 = (f32[1,512,4,4,128]{4,1,3,2,0:T(8,128)}, f32[1,512,4,128]{3,1,2,0:T(8,128)}, f32[1,512,4,128]{3,1,2,0:T(8,128)}) conditional(s32[]{:T(128)} %convert_element_type.133, (f32[1,512,4,4,128]{4,1,3,2,0:T(8,128)}, bf16[1,512,4,128]{3,1,2,0:T(8,128)(2,1)S(1)}, bf16[1,512,4,4,128]{4,1,3,2,0:T(8,128)(2,1)S(1)}, ...), branch_computations={%region_11.11_spmd, %region_12.12_spmd} | conditional | flops 2704146432 | bytes 105742448 | solution.py:99
  1266.6 32.2 %collective-permute-done.2 = bf16[1,512,4,128]{3,1,2,0:T(8,128)(2,1)S(1)} collective-permute-done((bf16[1,512,4,128]{3,1,2,0:T(8,128)(2,1)}, bf16[1,512,4,128]{3,1,2,0:T(8,128)(2,1)S(1)}, u32[]{:S(2)}, u32[]{:S(2)}) %collective-permute-start.2) | collective-permute-done | bytes 524320 | tf_op jit(solution)/shard_map/while/body/eval_jaxpr/ppermute | solution.py:94
  1305.2 15.2 %conditional.5 = (f32[1,512,4,4,128]{4,1,3,2,0:T(8,128)}, f32[1,512,4,128]{3,1,2,0:T(8,128)}, f32[1,512,4,128]{3,1,2,0:T(8,128)}) conditional(s32[]{:T(128)} %convert_element_type.133, (f32[1,512,4,4,128]{4,1,3,2,0:T(8,128)}, bf16[1,512,4,128]{3,1,2,0:T(8,128)(2,1)S(1)}, bf16[1,512,4,4,128]{4,1,3,2,0:T(8,128)(2,1)S(1)}, ...), branch_computations={%region_11.11_spmd, %region_12.12_spmd} | conditional | flops 2704146432 | bytes 105742448 | solution.py:99
  (644 shorter events, 1003.6 us)
Async XLA Ops:
  486.4 38.8 %collective-permute-start.4 = (f32[1,512,4,128]{3,1,2,0:T(8,128)}, f32[1,512,4,128]{3,1,2,0:T(8,128)}, u32[]{:S(2)}, u32[]{:S(2)}) collective-permute-start(f32[1,512,4,128]{3,1,2,0:T(8,128)} %get-tuple-element.878), channel_id=1, source_target_pairs={{0,1},{1,2},{2,3},{3,4},{4,5},{5,6},{6,7},{7,8},{8,9},{9,10},{10,1... | collective-permute-start | bytes 3145736 | tf_op jit(solution)/shard_map/while/body/eval_jaxpr/ppermute | solution.py:96
  486.5 38.7 %collective-permute-start.5 = (f32[1,512,4,128]{3,1,2,0:T(8,128)}, f32[1,512,4,128]{3,1,2,0:T(8,128)}, u32[]{:S(2)}, u32[]{:S(2)}) collective-permute-start(f32[1,512,4,128]{3,1,2,0:T(8,128)} %get-tuple-element.879), channel_id=1, source_target_pairs={{0,1},{1,2},{2,3},{3,4},{4,5},{5,6},{6,7},{7,8},{8,9},{9,10},{10,1... | collective-permute-start | bytes 3145736 | tf_op jit(solution)/shard_map/while/body/eval_jaxpr/ppermute | solution.py:97
  543.5 38.7 %collective-permute-start.4 = (f32[1,512,4,128]{3,1,2,0:T(8,128)}, f32[1,512,4,128]{3,1,2,0:T(8,128)}, u32[]{:S(2)}, u32[]{:S(2)}) collective-permute-start(f32[1,512,4,128]{3,1,2,0:T(8,128)} %get-tuple-element.878), channel_id=1, source_target_pairs={{0,1},{1,2},{2,3},{3,4},{4,5},{5,6},{6,7},{7,8},{8,9},{9,10},{10,1... | collective-permute-start | bytes 3145736 | tf_op jit(solution)/shard_map/while/body/eval_jaxpr/ppermute | solution.py:96
  543.5 38.7 %collective-permute-start.5 = (f32[1,512,4,128]{3,1,2,0:T(8,128)}, f32[1,512,4,128]{3,1,2,0:T(8,128)}, u32[]{:S(2)}, u32[]{:S(2)}) collective-permute-start(f32[1,512,4,128]{3,1,2,0:T(8,128)} %get-tuple-element.879), channel_id=1, source_target_pairs={{0,1},{1,2},{2,3},{3,4},{4,5},{5,6},{6,7},{7,8},{8,9},{9,10},{10,1... | collective-permute-start | bytes 3145736 | tf_op jit(solution)/shard_map/while/body/eval_jaxpr/ppermute | solution.py:97
  543.6 37.9 %collective-permute-start.3 = (bf16[1,512,4,128]{3,1,2,0:T(8,128)(2,1)}, bf16[1,512,4,128]{3,1,2,0:T(8,128)(2,1)S(1)}, u32[]{:S(2)}, u32[]{:S(2)}) collective-permute-start(bf16[1,512,4,128]{3,1,2,0:T(8,128)(2,1)} %get-tuple-element.881), channel_id=1, source_target_pairs={{0,1},{1,2},{2,3},{3,4},{4,5},{5,6},{6,7},{7,8},{8,9},{9,10},{10,1... | collective-permute-start | bytes 1572872 | tf_op jit(solution)/shard_map/while/body/eval_jaxpr/ppermute | solution.py:95
  600.6 38.7 %collective-permute-start.4 = (f32[1,512,4,128]{3,1,2,0:T(8,128)}, f32[1,512,4,128]{3,1,2,0:T(8,128)}, u32[]{:S(2)}, u32[]{:S(2)}) collective-permute-start(f32[1,512,4,128]{3,1,2,0:T(8,128)} %get-tuple-element.878), channel_id=1, source_target_pairs={{0,1},{1,2},{2,3},{3,4},{4,5},{5,6},{6,7},{7,8},{8,9},{9,10},{10,1... | collective-permute-start | bytes 3145736 | tf_op jit(solution)/shard_map/while/body/eval_jaxpr/ppermute | solution.py:96
  600.6 38.7 %collective-permute-start.5 = (f32[1,512,4,128]{3,1,2,0:T(8,128)}, f32[1,512,4,128]{3,1,2,0:T(8,128)}, u32[]{:S(2)}, u32[]{:S(2)}) collective-permute-start(f32[1,512,4,128]{3,1,2,0:T(8,128)} %get-tuple-element.879), channel_id=1, source_target_pairs={{0,1},{1,2},{2,3},{3,4},{4,5},{5,6},{6,7},{7,8},{8,9},{9,10},{10,1... | collective-permute-start | bytes 3145736 | tf_op jit(solution)/shard_map/while/body/eval_jaxpr/ppermute | solution.py:97
  600.6 37.9 %collective-permute-start.3 = (bf16[1,512,4,128]{3,1,2,0:T(8,128)(2,1)}, bf16[1,512,4,128]{3,1,2,0:T(8,128)(2,1)S(1)}, u32[]{:S(2)}, u32[]{:S(2)}) collective-permute-start(bf16[1,512,4,128]{3,1,2,0:T(8,128)(2,1)} %get-tuple-element.881), channel_id=1, source_target_pairs={{0,1},{1,2},{2,3},{3,4},{4,5},{5,6},{6,7},{7,8},{8,9},{9,10},{10,1... | collective-permute-start | bytes 1572872 | tf_op jit(solution)/shard_map/while/body/eval_jaxpr/ppermute | solution.py:95
  657.6 38.7 %collective-permute-start.4 = (f32[1,512,4,128]{3,1,2,0:T(8,128)}, f32[1,512,4,128]{3,1,2,0:T(8,128)}, u32[]{:S(2)}, u32[]{:S(2)}) collective-permute-start(f32[1,512,4,128]{3,1,2,0:T(8,128)} %get-tuple-element.878), channel_id=1, source_target_pairs={{0,1},{1,2},{2,3},{3,4},{4,5},{5,6},{6,7},{7,8},{8,9},{9,10},{10,1... | collective-permute-start | bytes 3145736 | tf_op jit(solution)/shard_map/while/body/eval_jaxpr/ppermute | solution.py:96
  657.6 38.7 %collective-permute-start.5 = (f32[1,512,4,128]{3,1,2,0:T(8,128)}, f32[1,512,4,128]{3,1,2,0:T(8,128)}, u32[]{:S(2)}, u32[]{:S(2)}) collective-permute-start(f32[1,512,4,128]{3,1,2,0:T(8,128)} %get-tuple-element.879), channel_id=1, source_target_pairs={{0,1},{1,2},{2,3},{3,4},{4,5},{5,6},{6,7},{7,8},{8,9},{9,10},{10,1... | collective-permute-start | bytes 3145736 | tf_op jit(solution)/shard_map/while/body/eval_jaxpr/ppermute | solution.py:97
  714.7 38.7 %collective-permute-start.4 = (f32[1,512,4,128]{3,1,2,0:T(8,128)}, f32[1,512,4,128]{3,1,2,0:T(8,128)}, u32[]{:S(2)}, u32[]{:S(2)}) collective-permute-start(f32[1,512,4,128]{3,1,2,0:T(8,128)} %get-tuple-element.878), channel_id=1, source_target_pairs={{0,1},{1,2},{2,3},{3,4},{4,5},{5,6},{6,7},{7,8},{8,9},{9,10},{10,1... | collective-permute-start | bytes 3145736 | tf_op jit(solution)/shard_map/while/body/eval_jaxpr/ppermute | solution.py:96
  714.7 38.7 %collective-permute-start.5 = (f32[1,512,4,128]{3,1,2,0:T(8,128)}, f32[1,512,4,128]{3,1,2,0:T(8,128)}, u32[]{:S(2)}, u32[]{:S(2)}) collective-permute-start(f32[1,512,4,128]{3,1,2,0:T(8,128)} %get-tuple-element.879), channel_id=1, source_target_pairs={{0,1},{1,2},{2,3},{3,4},{4,5},{5,6},{6,7},{7,8},{8,9},{9,10},{10,1... | collective-permute-start | bytes 3145736 | tf_op jit(solution)/shard_map/while/body/eval_jaxpr/ppermute | solution.py:97
  771.7 38.7 %collective-permute-start.4 = (f32[1,512,4,128]{3,1,2,0:T(8,128)}, f32[1,512,4,128]{3,1,2,0:T(8,128)}, u32[]{:S(2)}, u32[]{:S(2)}) collective-permute-start(f32[1,512,4,128]{3,1,2,0:T(8,128)} %get-tuple-element.878), channel_id=1, source_target_pairs={{0,1},{1,2},{2,3},{3,4},{4,5},{5,6},{6,7},{7,8},{8,9},{9,10},{10,1... | collective-permute-start | bytes 3145736 | tf_op jit(solution)/shard_map/while/body/eval_jaxpr/ppermute | solution.py:96
  771.7 38.7 %collective-permute-start.5 = (f32[1,512,4,128]{3,1,2,0:T(8,128)}, f32[1,512,4,128]{3,1,2,0:T(8,128)}, u32[]{:S(2)}, u32[]{:S(2)}) collective-permute-start(f32[1,512,4,128]{3,1,2,0:T(8,128)} %get-tuple-element.879), channel_id=1, source_target_pairs={{0,1},{1,2},{2,3},{3,4},{4,5},{5,6},{6,7},{7,8},{8,9},{9,10},{10,1... | collective-permute-start | bytes 3145736 | tf_op jit(solution)/shard_map/while/body/eval_jaxpr/ppermute | solution.py:97
  828.8 38.7 %collective-permute-start.4 = (f32[1,512,4,128]{3,1,2,0:T(8,128)}, f32[1,512,4,128]{3,1,2,0:T(8,128)}, u32[]{:S(2)}, u32[]{:S(2)}) collective-permute-start(f32[1,512,4,128]{3,1,2,0:T(8,128)} %get-tuple-element.878), channel_id=1, source_target_pairs={{0,1},{1,2},{2,3},{3,4},{4,5},{5,6},{6,7},{7,8},{8,9},{9,10},{10,1... | collective-permute-start | bytes 3145736 | tf_op jit(solution)/shard_map/while/body/eval_jaxpr/ppermute | solution.py:96
  828.8 38.7 %collective-permute-start.5 = (f32[1,512,4,128]{3,1,2,0:T(8,128)}, f32[1,512,4,128]{3,1,2,0:T(8,128)}, u32[]{:S(2)}, u32[]{:S(2)}) collective-permute-start(f32[1,512,4,128]{3,1,2,0:T(8,128)} %get-tuple-element.879), channel_id=1, source_target_pairs={{0,1},{1,2},{2,3},{3,4},{4,5},{5,6},{6,7},{7,8},{8,9},{9,10},{10,1... | collective-permute-start | bytes 3145736 | tf_op jit(solution)/shard_map/while/body/eval_jaxpr/ppermute | solution.py:97
  885.8 38.7 %collective-permute-start.4 = (f32[1,512,4,128]{3,1,2,0:T(8,128)}, f32[1,512,4,128]{3,1,2,0:T(8,128)}, u32[]{:S(2)}, u32[]{:S(2)}) collective-permute-start(f32[1,512,4,128]{3,1,2,0:T(8,128)} %get-tuple-element.878), channel_id=1, source_target_pairs={{0,1},{1,2},{2,3},{3,4},{4,5},{5,6},{6,7},{7,8},{8,9},{9,10},{10,1... | collective-permute-start | bytes 3145736 | tf_op jit(solution)/shard_map/while/body/eval_jaxpr/ppermute | solution.py:96
  885.8 38.7 %collective-permute-start.5 = (f32[1,512,4,128]{3,1,2,0:T(8,128)}, f32[1,512,4,128]{3,1,2,0:T(8,128)}, u32[]{:S(2)}, u32[]{:S(2)}) collective-permute-start(f32[1,512,4,128]{3,1,2,0:T(8,128)} %get-tuple-element.879), channel_id=1, source_target_pairs={{0,1},{1,2},{2,3},{3,4},{4,5},{5,6},{6,7},{7,8},{8,9},{9,10},{10,1... | collective-permute-start | bytes 3145736 | tf_op jit(solution)/shard_map/while/body/eval_jaxpr/ppermute | solution.py:97
  942.9 38.7 %collective-permute-start.4 = (f32[1,512,4,128]{3,1,2,0:T(8,128)}, f32[1,512,4,128]{3,1,2,0:T(8,128)}, u32[]{:S(2)}, u32[]{:S(2)}) collective-permute-start(f32[1,512,4,128]{3,1,2,0:T(8,128)} %get-tuple-element.878), channel_id=1, source_target_pairs={{0,1},{1,2},{2,3},{3,4},{4,5},{5,6},{6,7},{7,8},{8,9},{9,10},{10,1... | collective-permute-start | bytes 3145736 | tf_op jit(solution)/shard_map/while/body/eval_jaxpr/ppermute | solution.py:96
  942.9 38.7 %collective-permute-start.5 = (f32[1,512,4,128]{3,1,2,0:T(8,128)}, f32[1,512,4,128]{3,1,2,0:T(8,128)}, u32[]{:S(2)}, u32[]{:S(2)}) collective-permute-start(f32[1,512,4,128]{3,1,2,0:T(8,128)} %get-tuple-element.879), channel_id=1, source_target_pairs={{0,1},{1,2},{2,3},{3,4},{4,5},{5,6},{6,7},{7,8},{8,9},{9,10},{10,1... | collective-permute-start | bytes 3145736 | tf_op jit(solution)/shard_map/while/body/eval_jaxpr/ppermute | solution.py:97
  996.8 38.7 %collective-permute-start.4 = (f32[1,512,4,128]{3,1,2,0:T(8,128)}, f32[1,512,4,128]{3,1,2,0:T(8,128)}, u32[]{:S(2)}, u32[]{:S(2)}) collective-permute-start(f32[1,512,4,128]{3,1,2,0:T(8,128)} %get-tuple-element.878), channel_id=1, source_target_pairs={{0,1},{1,2},{2,3},{3,4},{4,5},{5,6},{6,7},{7,8},{8,9},{9,10},{10,1... | collective-permute-start | bytes 3145736 | tf_op jit(solution)/shard_map/while/body/eval_jaxpr/ppermute | solution.py:96
  996.8 38.7 %collective-permute-start.5 = (f32[1,512,4,128]{3,1,2,0:T(8,128)}, f32[1,512,4,128]{3,1,2,0:T(8,128)}, u32[]{:S(2)}, u32[]{:S(2)}) collective-permute-start(f32[1,512,4,128]{3,1,2,0:T(8,128)} %get-tuple-element.879), channel_id=1, source_target_pairs={{0,1},{1,2},{2,3},{3,4},{4,5},{5,6},{6,7},{7,8},{8,9},{9,10},{10,1... | collective-permute-start | bytes 3145736 | tf_op jit(solution)/shard_map/while/body/eval_jaxpr/ppermute | solution.py:97
  1050.7 38.7 %collective-permute-start.4 = (f32[1,512,4,128]{3,1,2,0:T(8,128)}, f32[1,512,4,128]{3,1,2,0:T(8,128)}, u32[]{:S(2)}, u32[]{:S(2)}) collective-permute-start(f32[1,512,4,128]{3,1,2,0:T(8,128)} %get-tuple-element.878), channel_id=1, source_target_pairs={{0,1},{1,2},{2,3},{3,4},{4,5},{5,6},{6,7},{7,8},{8,9},{9,10},{10,1... | collective-permute-start | bytes 3145736 | tf_op jit(solution)/shard_map/while/body/eval_jaxpr/ppermute | solution.py:96
  1050.8 38.7 %collective-permute-start.5 = (f32[1,512,4,128]{3,1,2,0:T(8,128)}, f32[1,512,4,128]{3,1,2,0:T(8,128)}, u32[]{:S(2)}, u32[]{:S(2)}) collective-permute-start(f32[1,512,4,128]{3,1,2,0:T(8,128)} %get-tuple-element.879), channel_id=1, source_target_pairs={{0,1},{1,2},{2,3},{3,4},{4,5},{5,6},{6,7},{7,8},{8,9},{9,10},{10,1... | collective-permute-start | bytes 3145736 | tf_op jit(solution)/shard_map/while/body/eval_jaxpr/ppermute | solution.py:97
  1104.7 38.7 %collective-permute-start.4 = (f32[1,512,4,128]{3,1,2,0:T(8,128)}, f32[1,512,4,128]{3,1,2,0:T(8,128)}, u32[]{:S(2)}, u32[]{:S(2)}) collective-permute-start(f32[1,512,4,128]{3,1,2,0:T(8,128)} %get-tuple-element.878), channel_id=1, source_target_pairs={{0,1},{1,2},{2,3},{3,4},{4,5},{5,6},{6,7},{7,8},{8,9},{9,10},{10,1... | collective-permute-start | bytes 3145736 | tf_op jit(solution)/shard_map/while/body/eval_jaxpr/ppermute | solution.py:96
  1104.7 38.7 %collective-permute-start.5 = (f32[1,512,4,128]{3,1,2,0:T(8,128)}, f32[1,512,4,128]{3,1,2,0:T(8,128)}, u32[]{:S(2)}, u32[]{:S(2)}) collective-permute-start(f32[1,512,4,128]{3,1,2,0:T(8,128)} %get-tuple-element.879), channel_id=1, source_target_pairs={{0,1},{1,2},{2,3},{3,4},{4,5},{5,6},{6,7},{7,8},{8,9},{9,10},{10,1... | collective-permute-start | bytes 3145736 | tf_op jit(solution)/shard_map/while/body/eval_jaxpr/ppermute | solution.py:97
  1158.6 38.7 %collective-permute-start.4 = (f32[1,512,4,128]{3,1,2,0:T(8,128)}, f32[1,512,4,128]{3,1,2,0:T(8,128)}, u32[]{:S(2)}, u32[]{:S(2)}) collective-permute-start(f32[1,512,4,128]{3,1,2,0:T(8,128)} %get-tuple-element.878), channel_id=1, source_target_pairs={{0,1},{1,2},{2,3},{3,4},{4,5},{5,6},{6,7},{7,8},{8,9},{9,10},{10,1... | collective-permute-start | bytes 3145736 | tf_op jit(solution)/shard_map/while/body/eval_jaxpr/ppermute | solution.py:96
  1158.6 38.7 %collective-permute-start.5 = (f32[1,512,4,128]{3,1,2,0:T(8,128)}, f32[1,512,4,128]{3,1,2,0:T(8,128)}, u32[]{:S(2)}, u32[]{:S(2)}) collective-permute-start(f32[1,512,4,128]{3,1,2,0:T(8,128)} %get-tuple-element.879), channel_id=1, source_target_pairs={{0,1},{1,2},{2,3},{3,4},{4,5},{5,6},{6,7},{7,8},{8,9},{9,10},{10,1... | collective-permute-start | bytes 3145736 | tf_op jit(solution)/shard_map/while/body/eval_jaxpr/ppermute | solution.py:97
  1212.5 38.7 %collective-permute-start.4 = (f32[1,512,4,128]{3,1,2,0:T(8,128)}, f32[1,512,4,128]{3,1,2,0:T(8,128)}, u32[]{:S(2)}, u32[]{:S(2)}) collective-permute-start(f32[1,512,4,128]{3,1,2,0:T(8,128)} %get-tuple-element.878), channel_id=1, source_target_pairs={{0,1},{1,2},{2,3},{3,4},{4,5},{5,6},{6,7},{7,8},{8,9},{9,10},{10,1... | collective-permute-start | bytes 3145736 | tf_op jit(solution)/shard_map/while/body/eval_jaxpr/ppermute | solution.py:96
  1212.5 38.7 %collective-permute-start.5 = (f32[1,512,4,128]{3,1,2,0:T(8,128)}, f32[1,512,4,128]{3,1,2,0:T(8,128)}, u32[]{:S(2)}, u32[]{:S(2)}) collective-permute-start(f32[1,512,4,128]{3,1,2,0:T(8,128)} %get-tuple-element.879), channel_id=1, source_target_pairs={{0,1},{1,2},{2,3},{3,4},{4,5},{5,6},{6,7},{7,8},{8,9},{9,10},{10,1... | collective-permute-start | bytes 3145736 | tf_op jit(solution)/shard_map/while/body/eval_jaxpr/ppermute | solution.py:97
  1266.5 38.7 %collective-permute-start.4 = (f32[1,512,4,128]{3,1,2,0:T(8,128)}, f32[1,512,4,128]{3,1,2,0:T(8,128)}, u32[]{:S(2)}, u32[]{:S(2)}) collective-permute-start(f32[1,512,4,128]{3,1,2,0:T(8,128)} %get-tuple-element.878), channel_id=1, source_target_pairs={{0,1},{1,2},{2,3},{3,4},{4,5},{5,6},{6,7},{7,8},{8,9},{9,10},{10,1... | collective-permute-start | bytes 3145736 | tf_op jit(solution)/shard_map/while/body/eval_jaxpr/ppermute | solution.py:96
  1266.5 38.7 %collective-permute-start.5 = (f32[1,512,4,128]{3,1,2,0:T(8,128)}, f32[1,512,4,128]{3,1,2,0:T(8,128)}, u32[]{:S(2)}, u32[]{:S(2)}) collective-permute-start(f32[1,512,4,128]{3,1,2,0:T(8,128)} %get-tuple-element.879), channel_id=1, source_target_pairs={{0,1},{1,2},{2,3},{3,4},{4,5},{5,6},{6,7},{7,8},{8,9},{9,10},{10,1... | collective-permute-start | bytes 3145736 | tf_op jit(solution)/shard_map/while/body/eval_jaxpr/ppermute | solution.py:97
  (131 other events, 1592.9 us)
where the time goes:
time: 1350 us; the launch traced here: 1340 us
  waiting for transfers between devices  790 us (59%)
  matrix products  296 us (22%)
  local copies, waits for them, and re-layouts  138 us (10%)
  other arithmetic  110 us (8%)
    ppermute x15, waiting for transfers between devices, bwd_step(): k_cur = lax.ppermute(k_cur, 'ctx', perm_next)  482 us
    ppermute x15, waiting for transfers between devices, fwd_step(): k_cur = lax.ppermute(k_cur, 'ctx', perm_next)  146 us
    ppermute x15, waiting for transfers between devices, fwd_step(): v_cur = lax.ppermute(v_cur, 'ctx', perm_next)  84.3 us
    ppermute x15, waiting for transfers between devices, bwd_step(): v_cur = lax.ppermute(v_cur, 'ctx', perm_next)  72.4 us
    dot_general x16, matrix products, fwd_update(): jnp.einsum('bhgqk,bkhd->bhgqd', prob_tile.astype(jnp.bfloat16), v_blk, pr...  60.5 us
    while x75, local copies, waits for them, and re-layouts  59.1 us
    dot_general x16, matrix products, bwd_block(): jnp.einsum('bhgqk,bqhgd->bkhd', prob_tile.astype(jnp.bfloat16), g_blk, pr...  58.5 us
    dot_general x16, matrix products, bwd_block(): jnp.einsum('bhgqk,bqhgd->bkhd', dscore_tile, q_blk, preferred_element_typ...  46 us
  transfers between devices with their start and end apart: 92, of which 61 were waited for; matrix products, arithmetic and copies ran while one was open for 3% of the time, Pallas kernels for 0%

commit v1 on v0

v1 whole, which is shorter than its diff:
```python
import functools
import math

import jax
import jax.numpy as jnp
from jax import lax
from jax.experimental import pallas as pl
from jax.experimental.pallas import tpu as pltpu
from jax.sharding import PartitionSpec as P

F32 = jnp.float32
BF16 = jnp.bfloat16
NEG = -1e30
MESH = pl.DeviceIdType.MESH
NT_DIMS = (((1,), (1,)), ((), ()))


def dot(a, b):
    return jnp.dot(a, b, preferred_element_type=F32)


def dot_nt(a, b):
    return lax.dot_general(a, b, NT_DIMS, preferred_element_type=F32)


def attention_kernel(
    chips, q_in, k_in, v_in, g_in, o_out, dq_out, dk_out, dv_out,
    qn, gn, kvb, oT, ms, ls, ob, rbuf, acc, dkb,
    in_loc, in_send, in_recv, ag_send, ag_recv, rs_send, rs_recv, out_loc, out_send, out_recv,
):
    q_mine = qn.shape[0]
    piece, dim = qn.shape[3], qn.shape[4]
    kv_mine = kvb.shape[1]
    group = q_mine // kv_mine
    half = chips // 2
    scale = dim ** -0.5
    cexp = scale * math.log2(math.e)
    keys = 2 * piece

    me = lax.axis_index("ctx")
    core = me % 2
    chip = me // 2
    other = 1 - core
    n_dev = 2 * chips
    partner = me + 1 - 2 * core
    up = (me + 2) % n_dev
    down = (me + n_dev - 2) % n_dev

    barrier = pltpu.get_barrier_semaphore()
    for neighbour in (partner, up, down):
        pl.semaphore_signal(barrier, inc=1, device_id={"ctx": neighbour}, device_id_type=MESH)
    pl.semaphore_wait(barrier, 3)

    kv_at = lambda ref, core_id: ref.at[pl.ds(kv_mine * core_id, kv_mine)]
    q_at = lambda ref, core_id: ref.at[pl.ds(q_mine * core_id, q_mine)]

    ins = (
        (k_in, kv_at, kvb.at[chip, :, 0, :, core]),
        (v_in, kv_at, kvb.at[chip, :, 1, :, core]),
        (q_in, q_at, qn.at[:, :, core]),
        (g_in, q_at, gn.at[:, :, core]),
    )

    def in_copies(n):
        src, at, dst = ins[n]
        local = pltpu.make_async_copy(at(src, core), dst, in_loc.at[n])
        remote = pltpu.make_async_remote_copy(
            src_ref=at(src, other), dst_ref=dst, send_sem=in_send.at[n], recv_sem=in_recv.at[n],
            device_id={"ctx": partner}, device_id_type=MESH)
        return local, remote

    def wait_in(n):
        local, remote = in_copies(n)
        local.wait()
        remote.wait()

    for n in range(4):
        local, remote = in_copies(n)
        local.start()
        remote.start()

    def ring_to(direction):
        return (me + n_dev + 2 - 4 * direction) % n_dev

    def ag_copy(b, h, direction, hop):
        return pltpu.make_async_remote_copy(
            src_ref=kvb.at[b, h], dst_ref=kvb.at[b, h],
            send_sem=ag_send.at[direction, h, hop - 1], recv_sem=ag_recv.at[direction, h, hop - 1],
            device_id={"ctx": ring_to(direction)}, device_id_type=MESH)

    def item(t):
        r = t % 4
        h = ((r + 1) // 2) % 2
        return t // 4, r, h, r % 2

    n_items = 4 * half - 2

    wait_in(0)
    wait_in(1)
    for r in range(4):
        ag_copy(chip, ((r + 1) // 2) % 2, r % 2, 1).start()

    def init_body(n, carry):
        gi, qc = n // 4, n % 4
        ms[gi, qc] = jnp.full((1, piece), NEG, F32)
        ls[gi, qc] = jnp.zeros((1, piece), F32)
        oT[gi, qc] = jnp.zeros((dim, piece), F32)
        return carry

    lax.fori_loop(0, q_mine * 4, init_body, 0)
    wait_in(2)
    wait_in(3)

    def visible(x, qc, width):
        k_idx = lax.broadcasted_iota(jnp.int32, (keys, width), 0)
        q_idx = lax.broadcasted_iota(jnp.int32, (keys, width), 1)
        if width > piece:
            q_idx = q_idx % piece
        in_high = (k_idx >= piece).astype(jnp.int32)
        k_pos = k_idx + x * (piece - keys * in_high)
        q_pos = q_idx + (piece * qc + x * (piece * (3 - 2 * qc)))
        return k_pos <= q_pos

    def fwd_step(b, h, x, qc, own):
        hi, co = qc // 2, qc % 2
        kk = kvb[b, h, 0, x].reshape(keys, dim)
        vv = kvb[b, h, 1, x].reshape(keys, dim)
        heads = [h * group + g for g in range(group)]
        q = jnp.concatenate([qn[gi, hi, co] for gi in heads], axis=0)
        s = dot_nt(kk, q)
        if own:
            s = jnp.where(visible(x, qc, group * piece), s, NEG)
        m0 = jnp.concatenate([ms[gi, qc] for gi in heads], axis=1)
        l0 = jnp.concatenate([ls[gi, qc] for gi in heads], axis=1)
        m1 = jnp.maximum(m0, jnp.max(s, axis=0, keepdims=True))
        p = jnp.exp2((s - m1) * cexp)
        decay = jnp.exp2((m0 - m1) * cexp)
        l1 = l0 * decay + jnp.sum(p, axis=0, keepdims=True)
        pv = dot(vv.T, p.astype(BF16))
        for g, gi in enumerate(heads):
            cols = slice(g * piece, (g + 1) * piece)
            ms[gi, qc] = m1[:, cols]
            ls[gi, qc] = l1[:, cols]
            oT[gi, qc] = oT[gi, qc] * decay[:, cols] + pv[:, cols]

    def bwd_step(b, h, x, qc, slot, own):
        hi, co = qc // 2, qc % 2
        kk = kvb[b, h, 0, x].reshape(keys, dim)
        vv = kvb[b, h, 1, x].reshape(keys, dim)
        k_t = kk.T
        mask = visible(x, qc, piece) if own else None
        dv = dk = None
        for g in range(group):
            gi = h * group + g
            q = qn[gi, hi, co]
            do = gn[gi, hi, co]
            s = dot_nt(kk, q)
            if own:
                s = jnp.where(mask, s, NEG)
            p = jnp.exp2(s * cexp - ms[gi, qc])
            dp = dot_nt(vv, do)
            ds = (p * (dp - ls[gi, qc])).astype(BF16)
            dv_part = dot(p.astype(BF16), do)
            dk_part = dot(ds, q)
            dv = dv_part if dv is None else dv + dv_part
            dk = dk_part if dk is None else dk + dk_part
            oT[gi, qc] += dot(k_t, ds)
        acc[slot, 0, x] += dk.reshape(2, piece, dim)
        acc[slot, 1, x] += dv.reshape(2, piece, dim)

    def far_steps(b, step):
        past = (b < chip).astype(jnp.int32)

        def body(w, carry):
            x = (1 - past) * (w // 2)
            qc = past * w + (1 - past) * (2 + w % 2)
            step(x, qc)
            return carry

        lax.fori_loop(0, 4, body, 0)

    def own_steps(step):
        def body(n, carry):
            x = n // 4
            step(x, n - 2 * x)
            return carry

        lax.fori_loop(0, 6, body, 0)

    def own_fwd(h, carry):
        own_steps(lambda x, qc: fwd_step(chip, h, x, qc, True))
        return carry

    lax.fori_loop(0, kv_mine, own_fwd, 0)

    def fwd_item(t, carry):
        j, r, h, direction = item(t)
        d = j + 1
        b = (chip + chips + (2 * direction - 1) * d) % chips
        ag_copy(b, h, direction, d).wait_recv()

        @pl.when(d < half - r // 2)
        def _():
            ag_copy(b, h, direction, d + 1).start()

        far_steps(b, lambda x, qc: fwd_step(b, h, x, qc, False))
        return carry

    lax.fori_loop(0, n_items, fwd_item, 0)

    def fwd_end(n, carry):
        gi, qc = n // 4, n % 4
        hi, co = qc // 2, qc % 2
        total = ls[gi, qc]
        o_t = oT[gi, qc] / total
        ob[gi, hi, co] = o_t.T.astype(BF16)
        do_t = gn[gi, hi, co].astype(F32).T
        ls[gi, qc] = jnp.sum(o_t.astype(BF16).astype(F32) * do_t, axis=0, keepdims=True)
        ms[gi, qc] = ms[gi, qc] * cexp + jnp.log(total) * math.log2(math.e)
        oT[gi, qc] = jnp.zeros((dim, piece), F32)
        return carry

    lax.fori_loop(0, q_mine * 4, fwd_end, 0)

    outs = (
        (o_out, q_at, lambda k: ob.at[:, :, k]),
        (dq_out, q_at, lambda k: ob.at[:, :, k]),
        (dk_out, kv_at, lambda k: dkb.at[0, :, :, k]),
        (dv_out, kv_at, lambda k: dkb.at[1, :, :, k]),
    )

    def out_copies(n):
        dst, at, src = outs[n]
        local = pltpu.make_async_copy(src(core), at(dst, core), out_loc.at[n])
        remote = pltpu.make_async_remote_copy(
            src_ref=src(other), dst_ref=at(dst, core), send_sem=out_send.at[n], recv_sem=out_recv.at[n],
            device_id={"ctx": partner}, device_id_type=MESH)
        return local, remote

    def start_out(n):
        local, remote = out_copies(n)
        local.start()
        remote.start()

    start_out(0)

    def rs_copy(b, h, direction, d, slot):
        return pltpu.make_async_remote_copy(
            src_ref=rbuf.at[b, h], dst_ref=rbuf.at[slot, h],
            send_sem=rs_send.at[direction, h, d - 1], recv_sem=rs_recv.at[direction, h, d - 1],
            device_id={"ctx": ring_to(1 - direction)}, device_id_type=MESH)

    def rs_item(t):
        j, r, h, direction = item(t)
        d = half - r // 2 - j
        b = (chip + chips + (2 * direction - 1) * d) % chips
        last = (d == 1).astype(jnp.int32)
        slot = b + last * direction * (chips - b)
        return j, h, direction, d, b, slot

    def bwd_item(t, carry):
        j, h, direction, d, b, slot = rs_item(t)
        acc[0] = jnp.zeros(acc.shape[1:], F32)
        far_steps(b, lambda x, qc: bwd_step(b, h, x, qc, 0, False))

        @pl.when(j == 0)
        def _():
            rbuf[b, h] = acc[0]

        @pl.when(j > 0)
        def _():
            rs_copy(b, h, direction, d + 1, b).wait_recv()
            rbuf[b, h] += acc[0]

        rs_copy(b, h, direction, d, slot).start()
        return carry

    lax.fori_loop(0, n_items, bwd_item, 0)

    def own_bwd(h, carry):
        acc[h] = jnp.zeros(acc.shape[1:], F32)
        own_steps(lambda x, qc: bwd_step(chip, h, x, qc, h, True))
        return carry

    lax.fori_loop(0, kv_mine, own_bwd, 0)

    def wait_out(n, received):
        local, remote = out_copies(n)
        local.wait()
        remote.wait_send()
        if received:
            remote.wait_recv()

    wait_out(0, True)

    def dq_end(n, carry):
        gi, qc = n // 4, n % 4
        ob[gi, qc // 2, qc % 2] = (oT[gi, qc] * scale).T.astype(BF16)
        return carry

    lax.fori_loop(0, q_mine * 4, dq_end, 0)
    start_out(1)

    def kv_end(h, carry):
        for direction in range(2):
            rs_copy(chip, h, direction, 1, chip).wait_recv()
        for kv in range(2):
            total = acc[h, kv] + rbuf[chip, h, kv] + rbuf[chips, h, kv]
            if kv == 0:
                total = total * scale
            dkb[kv, h] = total.astype(BF16)
        return carry

    lax.fori_loop(0, kv_mine, kv_end, 0)
    start_out(2)
    start_out(3)

    def drain(t, carry):
        j, h, direction, d, b, slot = rs_item(t)
        rs_copy(b, h, direction, d, slot).wait_send()
        return carry

    lax.fori_loop(0, n_items, drain, 0)

    def drain_ag(t, carry):
        j, r, h, direction = item(t)
        b = (chip + chips + (2 * direction - 1) * j) % chips
        ag_copy(b, h, direction, j + 1).wait_send()
        return carry

    lax.fori_loop(0, n_items, drain_ag, 0)
    for n in range(1, 4):
        wait_out(n, True)


def solution(mesh):
    chips = mesh.shape["ctx"] // 2
    block_spec = P("data", "ctx", None, None)

    def heads_first(x):
        _, tokens, heads, dim = x.shape
        return jnp.transpose(x[0], (1, 0, 2)).reshape(heads, 2, tokens // 2, dim)

    def tokens_first(x, like):
        _, tokens, heads, dim = like.shape
        return jnp.transpose(x.reshape(heads, tokens, dim), (1, 0, 2))[None]

    def local_attention(queries, keys_in, values_in, grad_out):
        _, tokens, q_heads, dim = queries.shape
        kv_heads = keys_in.shape[2]
        piece = tokens // 2
        q_mine, kv_mine = q_heads // 2, kv_heads // 2
        half = chips // 2
        dma = pltpu.SemaphoreType.DMA
        q_shape = jax.ShapeDtypeStruct((q_heads, 2, piece, dim), BF16)
        kv_shape = jax.ShapeDtypeStruct((kv_heads, 2, piece, dim), BF16)
        any_spec = pl.BlockSpec(memory_space=pl.ANY)
        outs = pl.pallas_call(
            functools.partial(attention_kernel, chips),
            out_shape=(q_shape, q_shape, kv_shape, kv_shape),
            in_specs=[any_spec] * 4,
            out_specs=(any_spec,) * 4,
            scratch_shapes=[
                pltpu.VMEM((q_mine, 2, 2, piece, dim), BF16),
                pltpu.VMEM((q_mine, 2, 2, piece, dim), BF16),
                pltpu.VMEM((chips, kv_mine, 2, 2, 2, piece, dim), BF16),
                pltpu.VMEM((q_mine, 4, dim, piece), F32),
                pltpu.VMEM((q_mine, 4, 1, piece), F32),
                pltpu.VMEM((q_mine, 4, 1, piece), F32),
                pltpu.VMEM((q_mine, 2, 2, piece, dim), BF16),
                pltpu.VMEM((chips + 1, kv_mine, 2, 2, 2, piece, dim), F32),
                pltpu.VMEM((kv_mine, 2, 2, 2, piece, dim), F32),
                pltpu.VMEM((2, kv_mine, 2, 2, piece, dim), BF16),
                dma((4,)), dma((4,)), dma((4,)),
                dma((2, kv_mine, half)), dma((2, kv_mine, half)),
                dma((2, kv_mine, half)), dma((2, kv_mine, half)),
                dma((4,)), dma((4,)), dma((4,)),
            ],
            compiler_params=pltpu.CompilerParams(
                collective_id=0, has_side_effects=True, vmem_limit_bytes=60 * 2**20),
            name="ring_attention",
        )(heads_first(queries), heads_first(keys_in), heads_first(values_in), heads_first(grad_out))
        likes = (queries, queries, keys_in, keys_in)
        return tuple(tokens_first(x, like) for x, like in zip(outs, likes))

    return jax.shard_map(local_attention, mesh=mesh, in_specs=(block_spec,) * 4, out_specs=(block_spec,) * 4, check_vma=False)
```

time: 1350 us -> 295 us (0.22)
  the two profiles are of different devices: /device:TPU:150 before, /device:TPU:21 now
where the time goes in v1:
time: 295 us; the launch traced here: 294 us
  Pallas kernels  277 us (94%)
  local copies, waits for them, and re-layouts  16.5 us (6%)
    pallas_call x1, Pallas kernels, local_attention(): pl.pallas_call(functools.partial(attention_kernel, chips), out_shape=(q_s...  277 us
    broadcast_in_dim x2, local copies, waits for them, and re-layouts, tokens_first(): return jnp.transpose(x.reshape(heads, tokens, dim), (1, 0, 2))[None]  8.79 us
    transpose x4, local copies, waits for them, and re-layouts, heads_first(): return jnp.transpose(x[0], (1, 0, 2)).reshape(heads, 2, tokens // 2, dim)  7.68 us

profile of v1, /device:TPU:21, one launch (start us, length us, event | category | flops | bytes accessed | tf_op | source)
XLA Modules:
  0.0 294.5 jit_solution(11207692872456845385)
XLA Ops:
  0.6 0.0 copy-start
  0.6 2.1 copy.9
  2.7 1.9 copy.10
  4.6 0.0 copy-done
  4.6 0.0 copy-start.1
  4.6 1.9 copy.8
  6.5 0.0 copy-done.1
  6.5 1.9 copy.11
  8.3 277.3 %ring_attention.1 = (bf16[16,2,256,128]{3,2,1,0:T(8,128)(2,1)}, bf16[16,2,256,128]{3,2,1,0:T(8,128)(2,1)}, bf16[4,2,256,128]{3,2,1,0:T(8,128)(2,1)}, bf16[4,2,256,128]{3,2,1,0:T(8,128)(2,1)}) custom-call(bf16[16,2,256,128]{3,2,1,0:T(8,128)(2,1)} %bitcast.36, bf16[4,2,256,128]{3,2,1,0:T(8,128)(2,1)} %bitcast.38, bf16[4,2,256,128]{3,2,1,0:T(8,128)(2,1)} %bitcast.39, ...), custom_call_target="tpu_custom_call" | custom-call | tf_op jit(solution)/shard_map/ring_attention/pallas_call | solution.py:358
  285.6 0.0 copy-start.2
  285.6 0.0 copy-start.3
  285.7 7.0 %copy_bitcast_fusion = (bf16[1,512,16,128]{3,2,1,0:T(8,128)(2,1)}, bf16[1,512,16,128]{3,2,1,0:T(8,128)(2,1)}) fusion(bf16[16,512,128]{2,1,0:T(8,128)(2,1)} %bitcast.43, bf16[16,512,128]{2,1,0:T(8,128)(2,1)} %bitcast.42), kind=kLoop, calls=%fused_computation | loop fusion | bytes 8388608 | tf_op jit(solution)/shard_map/broadcast_in_dim | solution.py:346
  292.7 0.0 copy-done.2
  292.7 0.0 copy-done.3
  292.7 1.8 copy_bitcast_fusion.2
Async XLA Ops:
  0.6 4.0 %copy-start = (bf16[1,512,16,128]{3,2,1,0:T(8,128)(2,1)S(1)}, bf16[1,512,16,128]{3,2,1,0:T(8,128)(2,1)}, u32[]{:S(2)}) copy-start(bf16[1,512,16,128]{3,2,1,0:T(8,128)(2,1)} %param.4) | copy-start | bytes 6291460
  4.6 1.9 copy-start.1
  285.6 7.0 %copy-start.2 = (bf16[4,2,256,128]{3,2,1,0:T(8,128)(2,1)S(1)}, bf16[4,2,256,128]{3,2,1,0:T(8,128)(2,1)}, u32[]{:S(2)}) copy-start(bf16[4,2,256,128]{3,2,1,0:T(8,128)(2,1)} %get-tuple-element.10) | copy-start | bytes 1572868
  285.6 7.0 %copy-start.3 = (bf16[4,2,256,128]{3,2,1,0:T(8,128)(2,1)S(1)}, bf16[4,2,256,128]{3,2,1,0:T(8,128)(2,1)}, u32[]{:S(2)}) copy-start(bf16[4,2,256,128]{3,2,1,0:T(8,128)(2,1)} %get-tuple-element.11) | copy-start | bytes 1572868
